TPU v7x, 512 devices: a 8x2x16 block of a 8x8x16 slice. The times are simulated.
512 devices in a mesh: groups: 2 (over y), seq: 16 (over z), exp: 8 (over x), tp: 2 (over core).
Axes of the slice: x: 8, y: 2, z: 16, core: 2. Of those that a mesh axis runs over, the one named last changes fastest.
The devices are a block of a 8x8x16 slice.
Arguments:
- attn_query: bfloat16 [8192, 1152], P(('groups', 'seq'), ('exp', 'tp')), parts along dimension 0, may hold values from -6 to 6
- fresh_keys: bfloat16 [8192, 1152], P(('groups', 'seq'), ('exp', 'tp')), parts along dimension 0, may hold values from -6 to 6
- fresh_values: bfloat16 [8192, 1152], P(('groups', 'seq'), ('exp', 'tp')), parts along dimension 0, may hold values from -6 to 6
- stale_keys: bfloat16 [8192, 1152], P(('groups', 'seq'), ('exp', 'tp')), parts along dimension 0, may hold values from -6 to 6
- stale_values: bfloat16 [8192, 1152], P(('groups', 'seq'), ('exp', 'tp')), parts along dimension 0, may hold values from -6 to 6
- block_flags: int32 [64], P(('groups', 'seq')), parts along dimension 0, may hold values 0 or 1
- moe_tokens: bfloat16 [65536, 1152], P(('groups', 'seq', 'exp', 'tp')), parts along dimension 0, may hold values from -6 to 6
- expert_ids: int32 [65536, 2], P(('groups', 'seq', 'exp', 'tp')), parts along dimension 0, may hold values from 0 to 15, all different within a row; in each aligned block of 128 rows (0 to 127, 128 to 255, ...) at most 20 rows name the same one
- gate_weights: float32 [65536, 2], P(('groups', 'seq', 'exp', 'tp')), parts along dimension 0, may hold values from 0.25 to 1
- up_weight: bfloat16 [16, 1152, 4608], P('seq', None, ('exp', 'tp')), may hold values from -0.1875 to 0.1875
- up_bias: float32 [16, 4608], P('seq', ('exp', 'tp')), may hold values from -3 to 3
- down_weight: bfloat16 [16, 4608, 1152], P('seq', ('exp', 'tp')), may hold values from -0.09375 to 0.09375
- down_bias: float32 [16, 1152], P('seq'), may hold values from -2 to 2
Outputs:
- attn_out: bfloat16 [8192, 1152], P(('groups', 'seq'), ('exp', 'tp')), parts along dimension 0
- moe_out: bfloat16 [65536, 1152], P(('groups', 'seq', 'exp', 'tp')), parts along dimension 0
There are 2 independent parts, one for each index of `groups`. A program takes and returns all parts, laid end to end along the dimension named above; an argument that names none is the same for every part. Nothing has to cross between parts.
Inputs may be any that keep to these rules, and one draw needn't show every extreme that they name: `expert_ids`: the 2 ids of a token differ. In the rows of one device no expert is named more than 20 times, and in every draw some expert is named exactly 20 times in some device's rows.
All inputs are finite; a program needn't handle non-finite values. No bound on the sum of `block_flags` on one device may be relied on, other than what follows from the above.
Results may differ from a plain program's by a relative error of at most 0.014.
Values may be sent and summed in bfloat16 or wider, within the bound.
No kernel may reach another device: no remote copies, remote signals or barrier semaphores. Data moves between devices by JAX's collectives and lax.ppermute only.
A program may use at most 64 MiB of HBM per device.

v0:
```python
import math
import jax
import jax.numpy as jnp
from jax import lax
from jax.sharding import PartitionSpec as P

HD = 72


def in_one_piece(arrays, axis, dim, along):
    widths = [a.shape[along] for a in arrays]
    both = jnp.concatenate(arrays, axis=along)
    result = lax.all_gather(both, axis, axis=dim, tiled=True)
    return tuple(jnp.split(result, [sum(widths[:k]) for k in range(1, len(widths))], axis=along))


def sent_to_all(value, axis):
    copies = jnp.broadcast_to(value, (lax.axis_size(axis), *value.shape))
    return lax.all_to_all(copies, axis, split_axis=0, concat_axis=0, tiled=True)


def laid_out(parts, dim):
    parts = jnp.moveaxis(parts, 0, dim)
    dims = parts.shape
    return parts.reshape(*dims[:dim], dims[dim] * dims[dim + 1], *dims[dim + 2 :])


def collect(value, axis, dim):
    parts = sent_to_all(value, axis)
    return laid_out(parts, dim)


def over_all(share, axis, dim, apply):
    everything = lax.all_gather(share, axis, axis=dim, tiled=True)
    return apply(everything, jnp.int32(0))


def in_blocks(value, dim, size):
    dims = value.shape
    parts = value.reshape(*dims[:dim], size, dims[dim] // size, *dims[dim + 1 :])
    return jnp.moveaxis(parts, dim, 0)


def summed_on_arrival(value, axis, dim):
    size = lax.axis_size(axis)
    parts = lax.all_to_all(in_blocks(value, dim, size), axis, 0, 0, tiled=True)
    return jnp.sum(parts.astype(jnp.float32), axis=0)


def grouped_exchange(value, axis, split_dim, concat_dim, work, item_dim, out_dim):

    def moved(group):
        return lax.all_to_all(group, axis, split_axis=split_dim, concat_axis=concat_dim, tiled=True)

    items = jax.tree.leaves(value)[0].shape[item_dim]
    ends = [items * k // 2 for k in range(2 + 1)] if items % 2 == 0 else [0, items]
    groups = [
        jax.tree.map(lambda a: lax.slice_in_dim(a, low, high, axis=item_dim), value)
        for low, high in zip(ends, ends[1:])
    ]
    arrived = [moved(group) for group in groups]
    made = [work(group) for group in arrived]
    return jax.tree.map(lambda *parts: jnp.concatenate(parts, axis=out_dim), *made)


def attention_part(attn_query, fresh_keys, fresh_values, stale_keys, stale_values, block_flags):
    length = attn_query.shape[0]
    heads_here = attn_query.shape[1] // HD
    row_flags = (jnp.repeat(block_flags, length // block_flags.shape[0]) == 1)[:, None]
    keys = jnp.where(row_flags, fresh_keys, stale_keys)
    values = jnp.where(row_flags, fresh_values, stale_values)
    queries = attn_query.reshape(length, heads_here, HD)
    scale = 1.0 / math.sqrt(HD)
    initial = (
        jnp.full((heads_here, length), -1e30, jnp.float32),
        jnp.zeros((heads_here, length), jnp.float32),
        jnp.zeros((heads_here, length, HD), jnp.float32),
    )
    carry = initial
    piece = in_one_piece((keys, values), "seq", 0, 1)
    count = piece[0].shape[0]
    width = math.gcd(count, 512)
    key_blocks = piece[0].reshape(count // width, width, heads_here, HD)
    value_blocks = piece[1].reshape(count // width, width, heads_here, HD)

    def advance(state, blocks):
        highest, totals, weighted = state
        key_block, value_block = blocks
        scores = (
            jnp.einsum("qhd,khd->hqk", queries, key_block, preferred_element_type=jnp.float32)
            * scale
        )
        new_high = jnp.maximum(highest, jnp.max(scores, axis=-1))
        rescale = jnp.exp(highest - new_high)
        probs = jnp.exp(scores - new_high[:, :, None])
        totals = totals * rescale + jnp.sum(probs, axis=-1)
        weighted = weighted * rescale[:, :, None] + jnp.einsum(
            "hqk,khd->hqd",
            probs.astype(jnp.bfloat16),
            value_block,
            preferred_element_type=jnp.float32,
        )
        return ((new_high, totals, weighted), None)

    carry, unused = lax.scan(advance, carry, (key_blocks, value_blocks))
    highest, totals, weighted = carry
    mixed = weighted / totals[:, :, None]
    return jnp.transpose(mixed, (1, 0, 2)).reshape(length, heads_here * HD).astype(jnp.bfloat16)


def expert_part(moe_tokens, expert_ids, gate_weights, up_weight, up_bias, down_weight, down_bias):
    tokens_here, width = moe_tokens.shape
    choose = expert_ids.shape[1]
    number = lax.axis_size("seq") * up_weight.shape[0]
    capacity = 5 * tokens_here // (2 * number)
    flat_ids = expert_ids.reshape(-1)
    hits = (flat_ids[:, None] == jnp.arange(number, dtype=jnp.int32)[None, :]).astype(jnp.int32)
    before = jnp.cumsum(hits, axis=0) - hits
    place = jnp.sum(before * hits, axis=1)
    slot = flat_ids * capacity + place
    slot_pairs = slot.reshape(tokens_here, choose)
    table = jnp.sum(
        (
            slot_pairs[None, :, :] == jnp.arange(number * capacity, dtype=jnp.int32)[:, None, None]
        ).astype(jnp.int32),
        axis=-1,
    )
    buffer = jnp.dot(
        table.astype(jnp.bfloat16), moe_tokens, preferred_element_type=jnp.float32
    ).astype(jnp.bfloat16)
    buffer = buffer.reshape(number, capacity, width)

    def expert_fn(received):
        sources, count = (received.shape[0], received.shape[1])
        flat_rows = received.reshape(sources * count, width)
        chip_rows = collect(flat_rows, "tp", 0)
        total_rows = chip_rows.shape[0]

        def project(piece):
            return jax.nn.gelu(
                jnp.dot(chip_rows, piece[0], preferred_element_type=jnp.float32) + piece[1]
            ).astype(jnp.bfloat16)

        hidden = over_all(
            (up_weight[0], up_bias[0][None, :].astype(jnp.bfloat16)),
            "exp",
            1,
            lambda piece, start: project((piece[0], piece[1].astype(jnp.float32))),
        )
        down_whole = lax.all_gather(down_weight[0], "exp", axis=0, tiled=True)
        hidden_rows = lax.slice_in_dim(
            hidden, 0, total_rows // lax.axis_size("tp") * lax.axis_size("tp"), axis=0
        )
        summed = summed_on_arrival(
            jnp.dot(hidden_rows, down_whole, preferred_element_type=jnp.float32).astype(
                jnp.bfloat16
            ),
            "tp",
            0,
        )
        result = (
            (summed + down_bias[0][None, :]).astype(jnp.bfloat16).reshape(sources, count, width)
        )
        return lax.all_to_all(result, "seq", split_axis=0, concat_axis=0, tiled=True)

    returned = grouped_exchange(buffer, "seq", 0, 0, expert_fn, 1, 1)
    flat_out = returned.reshape(number * capacity, width)
    picked = flat_out[slot].reshape(tokens_here, choose, width).astype(jnp.float32)
    combined = jnp.sum(picked * gate_weights[:, :, None], axis=1)
    return combined.astype(jnp.bfloat16)


def local(
    attn_query,
    fresh_keys,
    fresh_values,
    stale_keys,
    stale_values,
    block_flags,
    moe_tokens,
    expert_ids,
    gate_weights,
    up_weight,
    up_bias,
    down_weight,
    down_bias,
):
    attn_out = attention_part(
        attn_query, fresh_keys, fresh_values, stale_keys, stale_values, block_flags
    )
    moe_out = expert_part(
        moe_tokens, expert_ids, gate_weights, up_weight, up_bias, down_weight, down_bias
    )
    return (attn_out, moe_out)


def solution(mesh):
    in_specs = (
        P(("groups", "seq"), ("exp", "tp")),
        P(("groups", "seq"), ("exp", "tp")),
        P(("groups", "seq"), ("exp", "tp")),
        P(("groups", "seq"), ("exp", "tp")),
        P(("groups", "seq"), ("exp", "tp")),
        P(("groups", "seq")),
        P(("groups", "seq", "exp", "tp"), None),
        P(("groups", "seq", "exp", "tp"), None),
        P(("groups", "seq", "exp", "tp"), None),
        P("seq", None, ("exp", "tp")),
        P("seq", ("exp", "tp")),
        P("seq", ("exp", "tp"), None),
        P("seq", None),
    )
    out_specs = (P(("groups", "seq"), ("exp", "tp")), P(("groups", "seq", "exp", "tp"), None))
    return jax.shard_map(local, mesh=mesh, in_specs=in_specs, out_specs=out_specs, check_vma=False)
```

profile of v0, /device:TPU:68, one launch (start us, length us, event | category | flops | bytes accessed | tf_op | source)
XLA Modules:
  0.0 323.5 jit_solution(15727244440906299351)
XLA Ops:
  7.3 0.7 all-gather.8.cloned.1.call-update
  8.1 0.7 all-gather.10.cloned.1.call-update
  8.8 0.8 copy.29
  11.7 1.0 fusion.68
  12.7 78.3 %all_to_all.40 = bf16[16,10,1152]{2,1,0:T(8,128)(2,1)S(1)} all-to-all(bf16[16,10,1152]{2,1,0:T(8,128)(2,1)S(1)} %get-tuple-element.100), channel_id=1, replica_groups=mesh['groups'=2,'seq'=16,'exp'=8,'tp'=2] {'seq'}, dimensions={0} | all-to-all | bytes 737280 | tf_op jit(solution)/shard_map/all_to_all | solution.py:53
  91.0 4.0 %all-to-all-start.4 = ((bf16[16,10,1152]{2,1,0:T(8,128)(2,1)}), bf16[16,10,1152]{2,1,0:T(8,128)(2,1)S(1)}, u32[]{:S(2)}, u32[]{:S(2)}) async-start(bf16[16,10,1152]{2,1,0:T(8,128)(2,1)} %get-tuple-element.101), calls=%async_computation.4 | async-start | bytes 1179648 | tf_op jit(solution)/shard_map/all_to_all | solution.py:53
  95.2 0.6 pad_maximum_fusion.1
  95.9 1.3 dynamic-slice
  98.2 16.6 %all-reduce = bf16[2304]{0:T(1024)(128)(2,1)S(1)} all-reduce(bf16[2304]{0:T(1024)(128)(2,1)S(1)} %dynamic-update-slice), channel_id=1, replica_groups=mesh['groups'=2,'seq'=16,'exp'=8,'tp'=2] {'exp'}, use_global_device_ids=true, to_apply=%add | all-reduce | flops 2304 | bytes 9216
  115.0 9.9 %all-to-all-done.4 = bf16[16,10,1152]{2,1,0:T(8,128)(2,1)S(1)} async-done(((bf16[16,10,1152]{2,1,0:T(8,128)(2,1)}), bf16[16,10,1152]{2,1,0:T(8,128)(2,1)S(1)}, u32[]{:S(2)}, u32[]{:S(2)}) %all-to-all-start.4) | async-done | bytes 368672 | tf_op jit(solution)/shard_map/all_to_all | solution.py:53
  124.9 0.9 broadcast_in_dim.42
  125.8 3.6 %all-to-all-start.1 = ((bf16[2,160,1152]{2,1,0:T(8,128)(2,1)}), bf16[2,160,1152]{2,1,0:T(8,128)(2,1)S(1)}, u32[]{:S(2)}, u32[]{:S(2)}) async-start(bf16[2,160,1152]{2,1,0:T(8,128)(2,1)} %broadcast_in_dim.42), calls=%async_computation.1 | async-start | bytes 1474560 | tf_op jit(solution)/shard_map/all_to_all | solution.py:19
  129.5 1.7 all-to-all-done.1
  131.3 4.8 %fusion.38 = bf16[320,2304]{1,0:T(8,128)(2,1)S(1)} fusion(bf16[320,1152]{1,0:T(8,128)(2,1)S(1)} %bitcast.116, bf16[1,1152,2304]{1,2,0:T(8,128)(2,1)} %all-gather.8.cloned.1.call-done, f32[2304]{0:T(1024)S(1)} %add.105), kind=kOutput, calls=%fused_computation.41 | convolution fusion | flops 1706065920 | bytes 7529472 | tf_op jit(solution)/shard_map/dot_general | solution.py:141
  136.1 50.8 %all-gather.10.cloned.1.call-done = bf16[1,2304,1152]{2,1,0:T(8,128)(2,1)} async-done(((bf16[1,288,1152]{2,1,0:T(8,128)(2,1)}), bf16[1,2304,1152]{2,1,0:T(8,128)(2,1)}) %all-gather.10.cloned.1.call-update) | async-done | bytes 5308432 | tf_op jit(solution)/shard_map/all_gather | solution.py:150
  186.9 4.6 %fusion.53 = bf16[320,1152]{1,0:T(8,128)(2,1)S(1)} fusion(bf16[320,2304]{1,0:T(8,128)(2,1)S(1)} %fusion.38, bf16[1,2304,1152]{2,1,0:T(8,128)(2,1)} %all-gather.10.cloned.1.call-done), kind=kOutput, calls=%fused_computation.50 | convolution fusion | flops 1699061760 | bytes 7520256 | tf_op jit(solution)/shard_map/dot_general | solution.py:155
  191.5 4.3 %all_to_all.41 = bf16[2,160,1152]{2,1,0:T(8,128)(2,1)S(1)} all-to-all(bf16[2,160,1152]{2,1,0:T(8,128)(2,1)S(1)} %bitcast.118), channel_id=1, replica_groups=mesh['groups'=2,'seq'=16,'exp'=8,'tp'=2] {'tp'}, dimensions={0} | all-to-all | bytes 1474560 | tf_op jit(solution)/shard_map/all_to_all | solution.py:46
  195.8 0.9 broadcast_in_dim.43
  196.7 3.6 %all-to-all-start.5 = ((bf16[2,160,1152]{2,1,0:T(8,128)(2,1)}), bf16[2,160,1152]{2,1,0:T(8,128)(2,1)S(1)}, u32[]{:S(2)}, u32[]{:S(2)}) async-start(bf16[2,160,1152]{2,1,0:T(8,128)(2,1)} %broadcast_in_dim.43), calls=%async_computation.5 | async-start | bytes 1474560 | tf_op jit(solution)/shard_map/all_to_all | solution.py:19
  200.5 1.6 all-to-all-done.5
  202.1 4.8 %fusion.50 = bf16[320,2304]{1,0:T(8,128)(2,1)S(1)} fusion(bf16[320,1152]{1,0:T(8,128)(2,1)S(1)} %bitcast.115, bf16[1,1152,2304]{1,2,0:T(8,128)(2,1)} %all-gather.8.cloned.1.call-done, f32[2304]{0:T(1024)S(1)} %add.105), kind=kOutput, calls=%fused_computation.49 | convolution fusion | flops 1706065920 | bytes 7529472 | tf_op jit(solution)/shard_map/dot_general | solution.py:141
  206.9 4.6 %fusion.56 = bf16[320,1152]{1,0:T(8,128)(2,1)S(1)} fusion(bf16[320,2304]{1,0:T(8,128)(2,1)S(1)} %fusion.50, bf16[1,2304,1152]{2,1,0:T(8,128)(2,1)} %all-gather.10.cloned.1.call-done), kind=kOutput, calls=%fused_computation.51 | convolution fusion | flops 1699061760 | bytes 7520256 | tf_op jit(solution)/shard_map/dot_general | solution.py:155
  211.6 4.3 %all_to_all.42 = bf16[2,160,1152]{2,1,0:T(8,128)(2,1)S(1)} all-to-all(bf16[2,160,1152]{2,1,0:T(8,128)(2,1)S(1)} %bitcast.117), channel_id=1, replica_groups=mesh['groups'=2,'seq'=16,'exp'=8,'tp'=2] {'tp'}, dimensions={0} | all-to-all | bytes 1474560 | tf_op jit(solution)/shard_map/all_to_all | solution.py:46
  216.1 1.2 add_convert_fusion.1
  217.3 13.1 %all-to-all-start.3 = ((bf16[16,10,1152]{2,1,0:T(8,128)(2,1)}), bf16[16,10,1152]{2,1,0:T(8,128)(2,1)S(1)}, u32[]{:S(2)}, u32[]{:S(2)}) async-start(bf16[16,10,1152]{2,1,0:T(8,128)(2,1)} %get-tuple-element.104), calls=%async_computation.3 | async-start | bytes 1179648 | tf_op jit(solution)/shard_map/all_to_all | solution.py:164
  230.7 50.2 %all-gather.6.cloned.1.call-done = bf16[4096,144]{0,1:T(8,128)(2,1)} async-done(((bf16[256,144]{0,1:T(8,128)(2,1)}), bf16[4096,144]{0,1:T(8,128)(2,1)}) %all-gather.6.cloned.1.call-update) | async-done | bytes 1179664 | tf_op jit(solution)/shard_map/all_gather | solution.py:13
  280.9 1.3 fusion.67
  283.0 7.0 %all-to-all-start.7 = ((bf16[16,10,1152]{2,1,0:T(8,128)(2,1)}), bf16[16,10,1152]{2,1,0:T(8,128)(2,1)S(1)}, u32[]{:S(2)}, u32[]{:S(2)}) async-start(bf16[16,10,1152]{2,1,0:T(8,128)(2,1)} %get-tuple-element.105), calls=%async_computation.7 | async-start | bytes 1179648 | tf_op jit(solution)/shard_map/all_to_all | solution.py:164
  290.0 5.8 %while.15 = (s32[]{:T(128)}, f32[1,256]{1,0:T(1,128)S(1)}, f32[1,256]{1,0:T(1,128)S(1)}, f32[1,256,72]{1,2,0:T(8,128)S(1)}, bf16[8,512,1,72]{1,3,2,0:T(8,128)(2,...) while((s32[]{:T(128)}, f32[1,256]{1,0:T(1,128)S(1)}, ...), condition=%wide.region_3.4_spmd.clone, body=%wide.region_0.3_spmd.clone.sunk | while | flops 38591744 | bytes 1921137 | solution.py:105
  296.4 16.1 %all-to-all-done.7 = bf16[16,10,1152]{2,1,0:T(8,128)(2,1)S(1)} async-done(((bf16[16,10,1152]{2,1,0:T(8,128)(2,1)}), bf16[16,10,1152]{2,1,0:T(8,128)(2,1)S(1)}, u32[]{:S(2)}, u32[]{:S(2)}) %all-to-all-start.7) | async-done | bytes 368672 | tf_op jit(solution)/shard_map/all_to_all | solution.py:164
  312.9 1.3 gather_fusion
  314.8 2.2 multiply_reduce_fusion
  (117 shorter events, 11.3 us)
Async XLA Ops:
  7.2 3.9 %copy-start = (bf16[128,1152]{1,0:T(8,128)(2,1)S(1)}, bf16[128,1152]{1,0:T(8,128)(2,1)}, u32[]{:S(2)}) copy-start(bf16[128,1152]{1,0:T(8,128)(2,1)} %param.21) | copy-start | bytes 884740
  7.2 124.1 %all-gather.8.cloned.1.call-start = ((), (), s32[]{:S(2)}) async-start(), calls=%async_computation.9 | async-start | bytes 5971968 | tf_op jit(solution)/shard_map/all_gather | solution.py:34
  8.0 178.9 %all-gather.10.cloned.1.call-start = ((), (), s32[]{:S(2)}) async-start(), calls=%async_computation.10 | async-start | bytes 5971968 | tf_op jit(solution)/shard_map/all_gather | solution.py:150
  11.4 83.7 %copy-start.9 = (s32[2]{0:T(128)S(1)}, s32[2]{0:T(128)}, u32[]{:S(2)}) copy-start(s32[2]{0:T(128)} %param.20) | copy-start | bytes 28
  11.5 83.7 %copy-start.2 = (bf16[256,72]{0,1:T(8,128)(2,1)S(1)}, bf16[256,72]{0,1:T(8,128)(2,1)}, u32[]{:S(2)}) copy-start(bf16[256,72]{0,1:T(8,128)(2,1)} %param.16) | copy-start | bytes 110596
  11.5 83.7 %copy-start.3 = (bf16[256,72]{0,1:T(8,128)(2,1)S(1)}, bf16[256,72]{0,1:T(8,128)(2,1)}, u32[]{:S(2)}) copy-start(bf16[256,72]{0,1:T(8,128)(2,1)} %param.18) | copy-start | bytes 110596
  11.5 83.7 %copy-start.4 = (bf16[256,72]{0,1:T(8,128)(2,1)S(1)}, bf16[256,72]{0,1:T(8,128)(2,1)}, u32[]{:S(2)}) copy-start(bf16[256,72]{0,1:T(8,128)(2,1)} %param.17) | copy-start | bytes 110596
  11.5 83.7 %copy-start.5 = (bf16[256,72]{0,1:T(8,128)(2,1)S(1)}, bf16[256,72]{0,1:T(8,128)(2,1)}, u32[]{:S(2)}) copy-start(bf16[256,72]{0,1:T(8,128)(2,1)} %param.19) | copy-start | bytes 110596
  11.7 86.2 %copy-start.7 = (f32[1,288]{1,0:T(1,128)S(1)}, f32[1,288]{1,0:T(1,128)}, u32[]{:S(2)}) copy-start(f32[1,288]{1,0:T(1,128)} %param.25) | copy-start | bytes 3460
  11.7 103.1 %copy-start.6 = (f32[1,1152]{1,0:T(1,128)S(1)}, f32[1,1152]{1,0:T(1,128)}, u32[]{:S(2)}) copy-start(f32[1,1152]{1,0:T(1,128)} %param.27) | copy-start | bytes 13828
  91.0 33.9 %all-to-all-start.4 = ((bf16[16,10,1152]{2,1,0:T(8,128)(2,1)}), bf16[16,10,1152]{2,1,0:T(8,128)(2,1)S(1)}, u32[]{:S(2)}, u32[]{:S(2)}) async-start(bf16[16,10,1152]{2,1,0:T(8,128)(2,1)} %get-tuple-element.101), calls=%async_computation.4 | async-start | bytes 1179648 | tf_op jit(solution)/shard_map/all_to_all | solution.py:53
  95.0 185.9 %all-gather.6.cloned.1.call-start = ((), (), s32[]{:S(2)}) async-start(), calls=%async_computation.8 | async-start | bytes 1253376 | tf_op jit(solution)/shard_map/all_gather | solution.py:13
  125.8 5.4 %all-to-all-start.1 = ((bf16[2,160,1152]{2,1,0:T(8,128)(2,1)}), bf16[2,160,1152]{2,1,0:T(8,128)(2,1)S(1)}, u32[]{:S(2)}, u32[]{:S(2)}) async-start(bf16[2,160,1152]{2,1,0:T(8,128)(2,1)} %broadcast_in_dim.42), calls=%async_computation.1 | async-start | bytes 1474560 | tf_op jit(solution)/shard_map/all_to_all | solution.py:19
  196.7 5.4 %all-to-all-start.5 = ((bf16[2,160,1152]{2,1,0:T(8,128)(2,1)}), bf16[2,160,1152]{2,1,0:T(8,128)(2,1)S(1)}, u32[]{:S(2)}, u32[]{:S(2)}) async-start(bf16[2,160,1152]{2,1,0:T(8,128)(2,1)} %broadcast_in_dim.43), calls=%async_computation.5 | async-start | bytes 1474560 | tf_op jit(solution)/shard_map/all_to_all | solution.py:19
  216.0 14.6 %copy-start.8 = (f32[128,2]{0,1:T(2,128)S(1)}, f32[128,2]{0,1:T(2,128)}, u32[]{:S(2)}) copy-start(f32[128,2]{0,1:T(2,128)} %param.23) | copy-start | bytes 3076
  217.3 65.7 %all-to-all-start.3 = ((bf16[16,10,1152]{2,1,0:T(8,128)(2,1)}), bf16[16,10,1152]{2,1,0:T(8,128)(2,1)S(1)}, u32[]{:S(2)}, u32[]{:S(2)}) async-start(bf16[16,10,1152]{2,1,0:T(8,128)(2,1)} %get-tuple-element.104), calls=%async_computation.3 | async-start | bytes 1179648 | tf_op jit(solution)/shard_map/all_to_all | solution.py:164
  282.2 7.8 %copy-start.1 = (bf16[256,72]{0,1:T(8,128)(2,1)S(1)}, bf16[256,72]{0,1:T(8,128)(2,1)}, u32[]{:S(2)}) copy-start(bf16[256,72]{0,1:T(8,128)(2,1)} %param.15) | copy-start | bytes 110596
  283.0 29.5 %all-to-all-start.7 = ((bf16[16,10,1152]{2,1,0:T(8,128)(2,1)}), bf16[16,10,1152]{2,1,0:T(8,128)(2,1)S(1)}, u32[]{:S(2)}, u32[]{:S(2)}) async-start(bf16[16,10,1152]{2,1,0:T(8,128)(2,1)} %get-tuple-element.105), calls=%async_computation.7 | async-start | bytes 1179648 | tf_op jit(solution)/shard_map/all_to_all | solution.py:164
Sparse Core Ops, SparseCore 0:
  10.1 103.9 all-gather.7
  116.3 70.5 all-gather.9
  189.5 91.3 all-gather.5
where the time goes:
time: 324 us
  waiting for transfers between devices  132 us (41%)
  blocking collectives  104 us (32%)
  starting transfers between devices  31.4 us (10%)
  matrix products  23.4 us (7%)
  between operations  14.9 us (5%)
  local copies, waits for them, and re-layouts  10.9 us (3%)
  other arithmetic  7.12 us (2%)
    all_to_all x1, blocking collectives, moved(): lax.all_to_all(group, axis, split_axis=split_dim, concat_axis=concat_dim,...  78.3 us
    all_gather x1, waiting for transfers between devices, expert_fn(): down_whole = lax.all_gather(down_weight[0], 'exp', axis=0, tiled=True)  50.8 us
    all_gather x1, waiting for transfers between devices, in_one_piece(): result = lax.all_gather(both, axis, axis=dim, tiled=True)  50.2 us
    all_to_all x2, starting transfers between devices, expert_fn(): lax.all_to_all(result, 'seq', split_axis=0, concat_axis=0, tiled=True)  20.1 us
    unnamed x1, blocking collectives  16.6 us
    all_to_all x2, waiting for transfers between devices, expert_fn(): lax.all_to_all(result, 'seq', split_axis=0, concat_axis=0, tiled=True)  16.1 us
    all_to_all x1, waiting for transfers between devices, moved(): lax.all_to_all(group, axis, split_axis=split_dim, concat_axis=concat_dim,...  9.91 us
    dot_general x2, matrix products, project(): jnp.dot(chip_rows, piece[0], preferred_element_type=jnp.float32) + piece[1]  9.61 us
  transfers between devices with their start and end apart: 8, of which 6 were waited for; matrix products, arithmetic and copies ran while one was open for 11% of the time, Pallas kernels for 0%

commit v1 on v0

--- a/solution.py
+++ b/solution.py
@@ -5,6 +5,13 @@
 from jax.sharding import PartitionSpec as P
 
 HD = 72
+
+
+def store_row_in(sheet):
+    top = jnp.stack(tuple((sheet for _ in range(lax.psum(1, "exp")))))
+    met_up = lax.all_to_all(top, "exp", 0, 0)
+    row_out = jnp.concatenate(met_up, axis=0)
+    return row_out
 
 
 def in_one_piece(arrays, axis, dim, along):
@@ -147,7 +154,7 @@
             1,
             lambda piece, start: project((piece[0], piece[1].astype(jnp.float32))),
         )
-        down_whole = lax.all_gather(down_weight[0], "exp", axis=0, tiled=True)
+        down_whole = store_row_in(down_weight[0])
         hidden_rows = lax.slice_in_dim(
             hidden, 0, total_rows // lax.axis_size("tp") * lax.axis_size("tp"), axis=0
         )

time: 324 us -> 426 us (1.31)
  the two profiles are of different devices: /device:TPU:68 before, /device:TPU:80 now
where the time goes in v1:
time: 426 us; the launch traced here: 425 us
  blocking collectives  244 us (57%)
  waiting for transfers between devices  87.6 us (21%)
  starting transfers between devices  37.3 us (9%)
  matrix products  21.3 us (5%)
  between operations  15.1 us (4%)
  local copies, waits for them, and re-layouts  12.8 us (3%)
  other arithmetic  7.12 us (2%)
    unnamed x1, blocking collectives  152 us
    all_to_all x1, blocking collectives, moved(): lax.all_to_all(group, axis, split_axis=split_dim, concat_axis=concat_dim,...  78.3 us
    all_gather x1, waiting for transfers between devices, in_one_piece(): result = lax.all_gather(both, axis, axis=dim, tiled=True)  33.6 us
    all_to_all x1, waiting for transfers between devices, moved(): lax.all_to_all(group, axis, split_axis=split_dim, concat_axis=concat_dim,...  31.4 us
    all_to_all x2, starting transfers between devices, expert_fn(): lax.all_to_all(result, 'seq', split_axis=0, concat_axis=0, tiled=True)  22.1 us
    all_to_all x2, waiting for transfers between devices, expert_fn(): lax.all_to_all(result, 'seq', split_axis=0, concat_axis=0, tiled=True)  20.2 us
    dot_general x2, matrix products, expert_fn(): jnp.dot(hidden_rows, down_whole, preferred_element_type=jnp.float32)  16.7 us
    all_to_all x2, blocking collectives, summed_on_arrival(): parts = lax.all_to_all(in_blocks(value, dim, size), axis, 0, 0, tiled=True)  8.63 us
  transfers between devices with their start and end apart: 7, of which 4 were waited for; matrix products, arithmetic and copies ran while one was open for 8% of the time, Pallas kernels for 0%

profile of v1, /device:TPU:80, one launch (start us, length us, event | category | flops | bytes accessed | tf_op | source)
XLA Modules:
  0.0 425.4 jit_solution(9579306577807190297)
XLA Ops:
  7.2 0.8 copy.29
  8.3 0.6 reduce-window.6
  9.5 0.3 convolution_convert_fusion.2
  10.0 1.0 fusion.70
  11.0 78.3 %all_to_all.46 = bf16[16,10,1152]{2,1,0:T(8,128)(2,1)S(1)} all-to-all(bf16[16,10,1152]{2,1,0:T(8,128)(2,1)S(1)} %get-tuple-element.100), channel_id=1, replica_groups=mesh['groups'=2,'seq'=16,'exp'=8,'tp'=2] {'seq'}, dimensions={0} | all-to-all | bytes 737280 | tf_op jit(solution)/shard_map/all_to_all | solution.py:60
  89.6 4.3 %all_to_all.47 = bf16[2,160,1152]{2,1,0:T(8,128)(2,1)S(1)} all-to-all(bf16[2,160,1152]{2,1,0:T(8,128)(2,1)S(1)} %broadcast_in_dim.42), channel_id=1, replica_groups=mesh['groups'=2,'seq'=16,'exp'=8,'tp'=2] {'tp'}, dimensions={0} | all-to-all | bytes 1474560 | tf_op jit(solution)/shard_map/all_to_all | solution.py:26
  93.9 4.0 all-to-all-start.5
  98.0 0.7 all-gather.6.cloned.1.call-update
  98.7 31.4 %all-to-all-done.5 = bf16[16,10,1152]{2,1,0:T(8,128)(2,1)S(1)} async-done(((bf16[16,10,1152]{2,1,0:T(8,128)(2,1)}), bf16[16,10,1152]{2,1,0:T(8,128)(2,1)S(1)}, u32[]{:S(2)}, u32[]{:S(2)}) %all-to-all-start.5) | async-done | bytes 368672 | tf_op jit(solution)/shard_map/all_to_all | solution.py:60
  130.1 2.8 stack.4
  132.9 7.5 %all-to-all-start.2 = ((bf16[8,288,1152]{2,1,0:T(8,128)(2,1)}), bf16[8,288,1152]{2,1,0:T(8,128)(2,1)}, u32[]{:S(2)}, u32[]{:S(2)}) async-start(bf16[8,288,1152]{2,1,0:T(8,128)(2,1)} %stack.4), calls=%async_computation.2 | async-start | bytes 10616832 | tf_op jit(solution)/shard_map/all_to_all | solution.py:12
  140.6 0.6 pad_maximum_fusion.1
  141.3 1.3 dynamic-slice
  143.5 152.4 %all-reduce = bf16[2304]{0:T(1024)(128)(2,1)S(1)} all-reduce(bf16[2304]{0:T(1024)(128)(2,1)S(1)} %dynamic-update-slice), channel_id=1, replica_groups=mesh['groups'=2,'seq'=16,'exp'=8,'tp'=2] {'exp'}, use_global_device_ids=true, to_apply=%add | all-reduce | flops 2304 | bytes 9216
  296.1 8.4 %convolution_convert_fusion.1 = bf16[320,1152]{1,0:T(8,128)(2,1)S(1)} fusion(bf16[2304,1152]{1,0:T(8,128)(2,1)} %bitcast.9, bf16[320,1152]{1,0:T(8,128)(2,1)S(1)} %bitcast.112, bf16[1,1152,2304]{1,2,0:T(8,128)(2,1)} %all-gather.6.cloned.1.call-done, f32[2304]{0:T(1024)S(1)} %add.105), kind=kOutput, calls=%fused_computation.47 | convolution fusion | flops 3405127680 | bytes 12100608 | tf_op jit(solution)/shard_map/dot_general | solution.py:162
  304.5 4.3 %all_to_all.48 = bf16[2,160,1152]{2,1,0:T(8,128)(2,1)S(1)} all-to-all(bf16[2,160,1152]{2,1,0:T(8,128)(2,1)S(1)} %bitcast.115), channel_id=1, replica_groups=mesh['groups'=2,'seq'=16,'exp'=8,'tp'=2] {'tp'}, dimensions={0} | all-to-all | bytes 1474560 | tf_op jit(solution)/shard_map/all_to_all | solution.py:53
  308.8 0.9 broadcast_in_dim.43
  309.7 3.6 all-to-all-start.6
  313.5 1.6 all-to-all-done.6
  315.1 8.4 %convolution_convert_fusion = bf16[320,1152]{1,0:T(8,128)(2,1)S(1)} fusion(bf16[2304,1152]{1,0:T(8,128)(2,1)} %bitcast.9, bf16[320,1152]{1,0:T(8,128)(2,1)S(1)} %bitcast.113, bf16[1,1152,2304]{1,2,0:T(8,128)(2,1)} %all-gather.6.cloned.1.call-done, f32[2304]{0:T(1024)S(1)} %add.105), kind=kOutput, calls=%fused_computation.46 | convolution fusion | flops 3405127680 | bytes 12100608 | tf_op jit(solution)/shard_map/dot_general | solution.py:162
  323.5 4.3 %all_to_all.49 = bf16[2,160,1152]{2,1,0:T(8,128)(2,1)S(1)} all-to-all(bf16[2,160,1152]{2,1,0:T(8,128)(2,1)S(1)} %bitcast.114), channel_id=1, replica_groups=mesh['groups'=2,'seq'=16,'exp'=8,'tp'=2] {'tp'}, dimensions={0} | all-to-all | bytes 1474560 | tf_op jit(solution)/shard_map/all_to_all | solution.py:53
  328.1 1.2 add_convert_fusion.1
  329.2 13.2 %all-to-all-start.4 = ((bf16[16,10,1152]{2,1,0:T(8,128)(2,1)}), bf16[16,10,1152]{2,1,0:T(8,128)(2,1)S(1)}, u32[]{:S(2)}, u32[]{:S(2)}) async-start(bf16[16,10,1152]{2,1,0:T(8,128)(2,1)} %get-tuple-element.104), calls=%async_computation.4 | async-start | bytes 1179648 | tf_op jit(solution)/shard_map/all_to_all | solution.py:171
  342.8 33.6 %all-gather.4.cloned.1.call-done = bf16[4096,144]{0,1:T(8,128)(2,1)} async-done(((bf16[256,144]{0,1:T(8,128)(2,1)}), bf16[4096,144]{0,1:T(8,128)(2,1)}) %all-gather.4.cloned.1.call-update) | async-done | bytes 1179664 | tf_op jit(solution)/shard_map/all_gather | solution.py:20
  376.5 1.3 fusion.69
  378.6 8.9 %all-to-all-start.8 = ((bf16[16,10,1152]{2,1,0:T(8,128)(2,1)}), bf16[16,10,1152]{2,1,0:T(8,128)(2,1)S(1)}, u32[]{:S(2)}, u32[]{:S(2)}) async-start(bf16[16,10,1152]{2,1,0:T(8,128)(2,1)} %get-tuple-element.105), calls=%async_computation.8 | async-start | bytes 1179648 | tf_op jit(solution)/shard_map/all_to_all | solution.py:171
  387.5 5.8 %while.15 = (s32[]{:T(128)}, f32[1,256]{1,0:T(1,128)S(1)}, f32[1,256]{1,0:T(1,128)S(1)}, f32[1,256,72]{1,2,0:T(8,128)S(1)}, bf16[8,512,1,72]{1,3,2,0:T(8,128)(2,...) while((s32[]{:T(128)}, f32[1,256]{1,0:T(1,128)S(1)}, ...), condition=%wide.region_3.4_spmd.clone, body=%wide.region_0.3_spmd.clone.sunk | while | flops 38591744 | bytes 1921137 | solution.py:112
  393.3 0.6 fusion.54
  393.9 20.2 %all-to-all-done.8 = bf16[16,10,1152]{2,1,0:T(8,128)(2,1)S(1)} async-done(((bf16[16,10,1152]{2,1,0:T(8,128)(2,1)}), bf16[16,10,1152]{2,1,0:T(8,128)(2,1)S(1)}, u32[]{:S(2)}, u32[]{:S(2)}) %all-to-all-start.8) | async-done | bytes 368672 | tf_op jit(solution)/shard_map/all_to_all | solution.py:171
  414.5 1.3 gather_fusion
  415.7 0.6 reshape.165
  416.3 2.2 multiply_reduce_fusion
  (116 shorter events, 9.2 us)
Async XLA Ops:
  7.2 2.3 copy-start
  89.4 40.7 %copy-start.2 = (bf16[1,288,1152]{2,1,0:T(8,128)(2,1)S(1)}, bf16[1,288,1152]{2,1,0:T(8,128)(2,1)}, u32[]{:S(2)}) copy-start(bf16[1,288,1152]{2,1,0:T(8,128)(2,1)} %param.26) | copy-start | bytes 1990660
  93.9 36.2 %all-to-all-start.5 = ((bf16[16,10,1152]{2,1,0:T(8,128)(2,1)}), bf16[16,10,1152]{2,1,0:T(8,128)(2,1)S(1)}, u32[]{:S(2)}, u32[]{:S(2)}) async-start(bf16[16,10,1152]{2,1,0:T(8,128)(2,1)} %get-tuple-element.101), calls=%async_computation.5 | async-start | bytes 1179648 | tf_op jit(solution)/shard_map/all_to_all | solution.py:60
  97.9 198.2 %all-gather.6.cloned.1.call-start = ((), (), s32[]{:S(2)}) async-start(), calls=%async_computation.10 | async-start | bytes 5971968 | tf_op jit(solution)/shard_map/all_gather | solution.py:41
  132.9 7.6 %copy-start.10 = (s32[2]{0:T(128)S(1)}, s32[2]{0:T(128)}, u32[]{:S(2)}) copy-start(s32[2]{0:T(128)} %param.20) | copy-start | bytes 28
  132.9 7.7 %copy-start.3 = (bf16[256,72]{0,1:T(8,128)(2,1)S(1)}, bf16[256,72]{0,1:T(8,128)(2,1)}, u32[]{:S(2)}) copy-start(bf16[256,72]{0,1:T(8,128)(2,1)} %param.16) | copy-start | bytes 110596
  132.9 7.7 %copy-start.4 = (bf16[256,72]{0,1:T(8,128)(2,1)S(1)}, bf16[256,72]{0,1:T(8,128)(2,1)}, u32[]{:S(2)}) copy-start(bf16[256,72]{0,1:T(8,128)(2,1)} %param.18) | copy-start | bytes 110596
  132.9 7.7 %copy-start.5 = (bf16[256,72]{0,1:T(8,128)(2,1)S(1)}, bf16[256,72]{0,1:T(8,128)(2,1)}, u32[]{:S(2)}) copy-start(bf16[256,72]{0,1:T(8,128)(2,1)} %param.17) | copy-start | bytes 110596
  132.9 7.7 %copy-start.6 = (bf16[256,72]{0,1:T(8,128)(2,1)S(1)}, bf16[256,72]{0,1:T(8,128)(2,1)}, u32[]{:S(2)}) copy-start(bf16[256,72]{0,1:T(8,128)(2,1)} %param.19) | copy-start | bytes 110596
  132.9 10.3 %copy-start.8 = (f32[1,288]{1,0:T(1,128)S(1)}, f32[1,288]{1,0:T(1,128)}, u32[]{:S(2)}) copy-start(f32[1,288]{1,0:T(1,128)} %param.25) | copy-start | bytes 3460
  132.9 163.0 %copy-start.7 = (f32[1,1152]{1,0:T(1,128)S(1)}, f32[1,1152]{1,0:T(1,128)}, u32[]{:S(2)}) copy-start(f32[1,1152]{1,0:T(1,128)} %param.27) | copy-start | bytes 13828
  132.9 163.2 %all-to-all-start.2 = ((bf16[8,288,1152]{2,1,0:T(8,128)(2,1)}), bf16[8,288,1152]{2,1,0:T(8,128)(2,1)}, u32[]{:S(2)}, u32[]{:S(2)}) async-start(bf16[8,288,1152]{2,1,0:T(8,128)(2,1)} %stack.4), calls=%async_computation.2 | async-start | bytes 10616832 | tf_op jit(solution)/shard_map/all_to_all | solution.py:12
  140.4 236.1 %all-gather.4.cloned.1.call-start = ((), (), s32[]{:S(2)}) async-start(), calls=%async_computation.9 | async-start | bytes 1253376 | tf_op jit(solution)/shard_map/all_gather | solution.py:20
  309.7 5.4 %all-to-all-start.6 = ((bf16[2,160,1152]{2,1,0:T(8,128)(2,1)}), bf16[2,160,1152]{2,1,0:T(8,128)(2,1)S(1)}, u32[]{:S(2)}, u32[]{:S(2)}) async-start(bf16[2,160,1152]{2,1,0:T(8,128)(2,1)} %broadcast_in_dim.43), calls=%async_computation.6 | async-start | bytes 1474560 | tf_op jit(solution)/shard_map/all_to_all | solution.py:26
  328.0 14.7 %copy-start.9 = (f32[128,2]{0,1:T(2,128)S(1)}, f32[128,2]{0,1:T(2,128)}, u32[]{:S(2)}) copy-start(f32[128,2]{0,1:T(2,128)} %param.23) | copy-start | bytes 3076
  329.2 49.3 %all-to-all-start.4 = ((bf16[16,10,1152]{2,1,0:T(8,128)(2,1)}), bf16[16,10,1152]{2,1,0:T(8,128)(2,1)S(1)}, u32[]{:S(2)}, u32[]{:S(2)}) async-start(bf16[16,10,1152]{2,1,0:T(8,128)(2,1)} %get-tuple-element.104), calls=%async_computation.4 | async-start | bytes 1179648 | tf_op jit(solution)/shard_map/all_to_all | solution.py:171
  377.8 9.7 %copy-start.1 = (bf16[256,72]{0,1:T(8,128)(2,1)S(1)}, bf16[256,72]{0,1:T(8,128)(2,1)}, u32[]{:S(2)}) copy-start(bf16[256,72]{0,1:T(8,128)(2,1)} %param.15) | copy-start | bytes 110596
  378.6 35.5 %all-to-all-start.8 = ((bf16[16,10,1152]{2,1,0:T(8,128)(2,1)}), bf16[16,10,1152]{2,1,0:T(8,128)(2,1)S(1)}, u32[]{:S(2)}, u32[]{:S(2)}) async-start(bf16[16,10,1152]{2,1,0:T(8,128)(2,1)} %get-tuple-element.105), calls=%async_computation.8 | async-start | bytes 1179648 | tf_op jit(solution)/shard_map/all_to_all | solution.py:171
Sparse Core Ops, SparseCore 0:
  100.8 148.1 all-gather.5
  251.7 124.7 all-gather.3
